TPU v7x, 32 devices: a whole 2x2x4 slice. The times are simulated.
32 devices in a mesh: dp: 8 (over z, y), mp: 4 (over x, core).
Axes of the slice: x: 2, y: 2, z: 4, core: 2. Of those that a mesh axis runs over, the one named last changes fastest.
Arguments:
- slow_weights: float32 [1, 3584, 1024], P(None, None, 'mp'), may hold values from -6 to 6
- fast_weights: bfloat16 [8, 1, 3584, 1024], P('dp', None, None, 'mp'), may hold values from -64 to 64
- momentum: float32 [1, 3584, 1024], P(None, None, 'mp'), may hold values from -1.2 to 1.2
Outputs:
- slow_next: float32 [1, 3584, 1024], P(None, None, 'mp')
- momentum_next: float32 [1, 3584, 1024], P(None, None, 'mp')
- fast_next: bfloat16 [8, 1, 3584, 1024], P('dp', None, None, 'mp')
All inputs are finite; a program needn't handle non-finite values.
Results may differ from a plain program's by a relative error of at most 0.001.
Values sent between devices are 32-bit elements; how exact they have to be, the bound alone decides.
A program may use at most 64 MiB of HBM per device.

v0:
```python
import math

import jax
import jax.numpy as jnp
from jax import lax
from jax.sharding import PartitionSpec as P

MOMENTUM_RATE = 0.9
OUTER_RATE = 0.7
CLIP_LEVEL = 0.2
EPSILON = 1e-06


def apply_update(slow_part, momentum_part, pseudo, squares, max_norm):
    factor = jnp.minimum(1.0, max_norm / (jnp.sqrt(squares) + EPSILON))
    gradient = factor * pseudo
    momentum_next = MOMENTUM_RATE * momentum_part + gradient
    slow_next = slow_part - OUTER_RATE * (gradient + MOMENTUM_RATE * momentum_next)
    return (slow_next, momentum_next)


def body(slow_weights, fast_weights, momentum):
    difference = slow_weights - fast_weights[0].astype(jnp.float32)
    replicas = lax.axis_size("dp")
    entries = (
        slow_weights.shape[0] * slow_weights.shape[1] * slow_weights.shape[2] * lax.axis_size("mp")
    )
    max_norm = CLIP_LEVEL * math.sqrt(entries)
    pseudo = lax.psum(difference, "dp") / replicas
    squares = lax.psum(jnp.sum(pseudo * pseudo), "mp")
    slow_next, momentum_next = apply_update(slow_weights, momentum, pseudo, squares, max_norm)
    fast_next = slow_next.astype(jnp.bfloat16)[None]
    return (slow_next, momentum_next, fast_next)


def solution(mesh):
    in_specs = (P(None, None, "mp"), P("dp", None, None, "mp"), P(None, None, "mp"))
    out_specs = (P(None, None, "mp"), P(None, None, "mp"), P("dp", None, None, "mp"))
    return jax.shard_map(body, mesh=mesh, in_specs=in_specs, out_specs=out_specs, check_vma=False)
```

profile of v0, /device:TPU:0, one launch (start us, length us, event | category | flops | bytes accessed | tf_op | source)
XLA Modules:
  0.0 184.9 jit_solution(11704129445931743159)
XLA Ops:
  7.2 0.0 all-reduce.2.cloned.1.call-start
  7.2 4.8 %convert_subtract_fusion = f32[1,3584,256]{2,1,0:T(8,128)} fusion(f32[1,3584,256]{2,1,0:T(8,128)} %param.3, bf16[1,1,3584,256]{3,2,1,0:T(8,128)(2,1)} %param.4), kind=kLoop, calls=%fused_computation | loop fusion | flops 1835008 | bytes 9175040 | tf_op jit(solution)/shard_map/sub | solution.py:23
  12.0 0.0 all-reduce.2.cloned.1.call-update
  12.0 145.8 %all-reduce.2.cloned.1.call-done = f32[1,3584,256]{2,1,0:T(8,128)} async-done(((f32[1,3584,256]{2,1,0:T(8,128)}), f32[1,3584,256]{2,1,0:T(8,128)}) %all-reduce.2.cloned.1.call-update) | async-done | bytes 3670032 | tf_op jit(solution)/shard_map/psum | solution.py:29
  157.8 3.6 %multiply_reduce_fusion = f32[]{:T(128)} fusion(f32[1,3584,256]{2,1,0:T(8,128)} %all-reduce.2.cloned.1.call-done), kind=kLoop, calls=%fused_computation.3 | loop fusion | flops 2752511 | bytes 3670020 | tf_op jit(solution)/shard_map/reduce_sum | solution.py:30
  161.4 7.0 %psum.15 = f32[]{:T(128)} all-reduce(f32[]{:T(128)} %multiply_reduce_fusion), channel_id=1, replica_groups=mesh['dp'=8,'mp'=4] {'mp'}, use_global_device_ids=true, to_apply=%region_2.0 | all-reduce | flops 1 | bytes 8 | tf_op jit(solution)/shard_map/psum | solution.py:30
  169.2 8.9 %convert_bitcast_fusion = (bf16[1,1,3584,256]{3,2,1,0:T(8,128)(2,1)}, f32[1,3584,256]{2,1,0:T(8,128)}, f32[1,3584,256]{2,1,0:T(8,128)}) fusion(f32[1,3584,256]{2,1,0:T(8,128)} %param.3, f32[1,3584,256]{2,1,0:T(8,128)} %all-reduce.2.cloned.1.call-done, f32[]{:T(128)S(6)} %mul.24, f32[1,3584,256]{2,1,0:T(8,128)} %param.5), kind=kLoop, calls=%fused_computation.4 | loop fusion | flops 7340032 | bytes 20185092 | tf_op jit(solution)/shard_map/broadcast_in_dim | solution.py:32
Async XLA Ops:
  7.2 150.7 %all-reduce.2.cloned.1.call-start = ((), (), s32[]{:S(2)}) async-start(), calls=%async_computation | async-start | bytes 7340032 | tf_op jit(solution)/shard_map/psum | solution.py:29
Sparse Core Ops, SparseCore 0:
  12.2 145.5 all-reduce.1
where the time goes:
time: 185 us
  waiting for transfers between devices  146 us (79%)
  other arithmetic  17.3 us (9%)
  between operations  14.8 us (8%)
  blocking collectives  7 us (4%)
    psum x1, waiting for transfers between devices, body(): pseudo = lax.psum(difference, 'dp') / replicas  146 us
    broadcast_in_dim x1, other arithmetic, body(): fast_next = slow_next.astype(jnp.bfloat16)[None]  8.86 us
    psum x1, blocking collectives, body(): squares = lax.psum(jnp.sum(pseudo * pseudo), 'mp')  7 us
    sub x1, other arithmetic, body(): difference = slow_weights - fast_weights[0].astype(jnp.float32)  4.8 us
  transfers between devices with their start and end apart: 1, of which 1 were waited for; matrix products, arithmetic and copies ran while one was open for 0% of the time, Pallas kernels for 0%

commit v1 on v0

v1 whole, which is shorter than its diff:
```python
import functools
import math

import jax
import jax.numpy as jnp
from jax import lax
from jax.experimental import pallas as pl
from jax.experimental.pallas import tpu as pltpu
from jax.sharding import PartitionSpec as P

MOMENTUM_RATE = 0.9
OUTER_RATE = 0.7
CLIP_LEVEL = 0.2
EPSILON = 1e-06
MESH = pl.DeviceIdType.MESH
SUBS = 4


def device_at(place, n):
    half = n // 2
    up = 2 * place
    down = 2 * (n - 1 - place) + 1
    return jnp.where(place < half, up, down)


def kernel(n, m, subs, max_norm, slow_ref, fast_ref, pseudo_ref, factor_ref,
           ring, squares, norms, send_sem, recv_sem, norm_send, norm_recv):
    rows, cols = slow_ref.shape
    chunk = rows // n
    sub = chunk // subs
    half = cols // 2
    me = lax.axis_index("dp")
    mine = lax.axis_index("mp")
    z, y = me // 2, lax.rem(me, 2)
    place = jnp.where(y == 0, z, n - 1 - z)
    right = device_at(lax.rem(place + 1, n), n)
    left = device_at(lax.rem(place + n - 1, n), n)
    goal = (right, left)
    order = (place, lax.rem(n - place, n))

    barrier = pltpu.get_barrier_semaphore()
    for other in (left, right):
        pl.semaphore_signal(barrier, inc=1, device_id={"dp": other}, device_id_type=MESH)
    for k in range(1, m):
        pl.semaphore_signal(
            barrier, inc=1, device_id={"mp": lax.rem(mine + k, m)}, device_id_type=MESH
        )

    def start_row(c, b):
        return pl.multiple_of(c * chunk + b * sub, sub)

    def own(d, b, c):
        at = (pl.ds(start_row(c, b), sub), pl.ds(d * half, half))
        return slow_ref[at] - fast_ref[at].astype(jnp.float32)

    def reduce_copy(d, b, s):
        return pltpu.make_async_remote_copy(
            src_ref=ring.at[d, b, s], dst_ref=ring.at[d, b, s + 1],
            send_sem=send_sem.at[d, b, s], recv_sem=recv_sem.at[d, b, s],
            device_id={"dp": goal[d]}, device_id_type=MESH,
        )

    def gather_copy(d, b, s, c):
        at = (pl.ds(start_row(c, b), sub), pl.ds(d * half, half))
        return pltpu.make_async_remote_copy(
            src_ref=pseudo_ref.at[at], dst_ref=pseudo_ref.at[at],
            send_sem=send_sem.at[d, b, n - 1 + s], recv_sem=recv_sem.at[d, b, n - 1 + s],
            device_id={"dp": goal[d]}, device_id_type=MESH,
        )

    def add_squares(d, b, c, value):
        sq = value * value
        squares[d, b, c] = jnp.sum(sq.reshape(sub // 8, 8, half), axis=0)

    streams = [(d, b) for b in range(subs) for d in range(2)]
    for d, b in streams:
        ring[d, b, 0] = own(d, b, order[d])
    pl.semaphore_wait(barrier, 2 + m - 1)
    for d, b in streams:
        reduce_copy(d, b, 0).start()

    def reduce_step(s, carry):
        for d, b in streams:
            reduce_copy(d, b, s).wait_recv()
            c = lax.rem(order[d] - s - 1 + n, n)
            ring[d, b, s + 1] = ring[d, b, s + 1] + own(d, b, c)
            reduce_copy(d, b, s + 1).start()
        return carry

    lax.fori_loop(0, n - 2, reduce_step, 0)
    for d, b in streams:
        reduce_copy(d, b, n - 2).wait_recv()
        c = lax.rem(order[d] + 1, n)
        value = (ring[d, b, n - 1] + own(d, b, c)) / n
        pseudo_ref[pl.ds(start_row(c, b), sub), pl.ds(d * half, half)] = value
        gather_copy(d, b, 0, c).start()
        add_squares(d, b, c, value)

    def gather_step(s, carry):
        for d, b in streams:
            c = lax.rem(order[d] - s + n, n)
            gather_copy(d, b, s, c).wait_recv()
            gather_copy(d, b, s + 1, c).start()
            at = (pl.ds(start_row(c, b), sub), pl.ds(d * half, half))
            add_squares(d, b, c, pseudo_ref[at])
        return carry

    lax.fori_loop(0, n - 2, gather_step, 0)
    for d, b in streams:
        c = lax.rem(order[d] + 2, n)
        gather_copy(d, b, n - 2, c).wait_recv()
        at = (pl.ds(start_row(c, b), sub), pl.ds(d * half, half))
        add_squares(d, b, c, pseudo_ref[at])

    part = jnp.sum(squares[...].reshape(2 * subs * n, 8, half), axis=0)
    norms[mine] = part

    def norm_copy(k):
        return pltpu.make_async_remote_copy(
            src_ref=norms.at[mine], dst_ref=norms.at[mine],
            send_sem=norm_send.at[k], recv_sem=norm_recv.at[k],
            device_id={"mp": lax.rem(mine + k, m)}, device_id_type=MESH,
        )

    for k in range(1, m):
        norm_copy(k).start()

    def drain(s, carry):
        for d, b in streams:
            reduce_copy(d, b, s).wait_send()
            gather_copy(d, b, s, 0).wait_send()
        return carry

    lax.fori_loop(0, n - 1, drain, 0)
    for k in range(1, m):
        norm_copy(k).wait_recv()
    total = norms[0]
    for j in range(1, m):
        total = total + norms[j]
    total = jnp.sum(jnp.sum(total, axis=1, keepdims=True), axis=0, keepdims=True)
    factor = jnp.minimum(1.0, max_norm / (jnp.sqrt(total) + EPSILON))
    factor_ref[...] = jnp.broadcast_to(factor, factor_ref.shape)
    for k in range(1, m):
        norm_copy(k).wait_send()


def body(slow_weights, fast_weights, momentum):
    n, m = lax.axis_size("dp"), lax.axis_size("mp")
    layers, depth, cols = slow_weights.shape
    rows = layers * depth
    max_norm = CLIP_LEVEL * math.sqrt(rows * cols * m)
    subs = SUBS
    while rows % (n * subs * 16):
        subs -= 1
    sub = rows // (n * subs)
    slow = slow_weights.reshape(rows, cols)
    vmem = pl.BlockSpec(memory_space=pltpu.VMEM)
    pseudo, factor = pl.pallas_call(
        functools.partial(kernel, n, m, subs, max_norm),
        out_shape=(
            jax.ShapeDtypeStruct((rows, cols), jnp.float32),
            jax.ShapeDtypeStruct((8, 128), jnp.float32),
        ),
        in_specs=[vmem, vmem],
        out_specs=(vmem, vmem),
        scratch_shapes=[
            pltpu.VMEM((2, subs, n, sub, cols // 2), jnp.float32),
            pltpu.VMEM((2, subs, n, 8, cols // 2), jnp.float32),
            pltpu.VMEM((m, 8, cols // 2), jnp.float32),
            pltpu.SemaphoreType.DMA((2, subs, 2 * n - 2)),
            pltpu.SemaphoreType.DMA((2, subs, 2 * n - 2)),
            pltpu.SemaphoreType.DMA((m,)),
            pltpu.SemaphoreType.DMA((m,)),
        ],
        compiler_params=pltpu.CompilerParams(collective_id=0, has_side_effects=True),
        name="ring",
    )(slow, fast_weights.reshape(rows, cols))
    gradient = factor[0, 0] * pseudo
    momentum_next = MOMENTUM_RATE * momentum.reshape(rows, cols) + gradient
    slow_next = slow - OUTER_RATE * (gradient + MOMENTUM_RATE * momentum_next)
    fast_next = slow_next.astype(jnp.bfloat16).reshape(fast_weights.shape)
    return (
        slow_next.reshape(slow_weights.shape),
        momentum_next.reshape(slow_weights.shape),
        fast_next,
    )


def solution(mesh):
    in_specs = (P(None, None, "mp"), P("dp", None, None, "mp"), P(None, None, "mp"))
    out_specs = (P(None, None, "mp"), P(None, None, "mp"), P("dp", None, None, "mp"))
    return jax.shard_map(body, mesh=mesh, in_specs=in_specs, out_specs=out_specs, check_vma=False)
```

time: 185 us -> 95.1 us (0.51)
  waiting for transfers between devices: 146 us -> 0 us
  Pallas kernels: 0 us -> 83.6 us
  between operations: 14.8 us -> 0.64 us
  other arithmetic: 17.3 us -> 9.43 us
  blocking collectives: 7 us -> 0 us
    psum x1 -> x0, waiting for transfers between devices: 146 us -> none  [body(): pseudo = lax.psum(difference, 'dp') / replicas]
    pallas_call x0 -> x1, Pallas kernels: none -> 83.6 us  [body(): pl.pallas_call(functools.partial(kernel, n, m, subs, max_norm), out_shape...]
    reshape x0 -> x1, other arithmetic: none -> 9.43 us  [body(): fast_next = slow_next.astype(jnp.bfloat16).reshape(fast_weights.shape)]
    broadcast_in_dim x1 -> x0, other arithmetic: 8.86 us -> none  [body(): fast_next = slow_next.astype(jnp.bfloat16)[None]]
    psum x1 -> x0, blocking collectives: 7 us -> none  [body(): squares = lax.psum(jnp.sum(pseudo * pseudo), 'mp')]
    sub x1 -> x0, other arithmetic: 4.8 us -> none  [body(): difference = slow_weights - fast_weights[0].astype(jnp.float32)]
    reduce_sum x1 -> x0, other arithmetic: 3.59 us -> none  [body(): squares = lax.psum(jnp.sum(pseudo * pseudo), 'mp')]
  transfers between devices with their start and end apart: 1 -> 0, of which waited for: 1 -> 0; matrix products, arithmetic and copies ran while one was open for 0% -> 0% of each run, Pallas kernels for 0% -> 0%
where the time goes in v1:
time: 95.1 us; the launch traced here: 94.9 us
  Pallas kernels  83.6 us (88%)
  other arithmetic  9.43 us (10%)
  local copies, waits for them, and re-layouts  1.2 us (1%)
    pallas_call x1, Pallas kernels, body(): pl.pallas_call(functools.partial(kernel, n, m, subs, max_norm), out_shape...  83.6 us
    reshape x1, other arithmetic, body(): fast_next = slow_next.astype(jnp.bfloat16).reshape(fast_weights.shape)  9.43 us

profile of v1, /device:TPU:0, one launch (start us, length us, event | category | flops | bytes accessed | tf_op | source)
XLA Modules:
  0.0 94.9 jit_solution(14145966407898164030)
XLA Ops:
  0.6 83.6 %ring.1 = (f32[3584,256]{1,0:T(8,128)}, f32[8,128]{1,0:T(8,128)}) custom-call(f32[3584,256]{1,0:T(8,128)} %bitcast.17, bf16[3584,256]{1,0:T(8,128)(2,1)} %bitcast.19), custom_call_target="tpu_custom_call" | custom-call | tf_op jit(solution)/shard_map/ring/pallas_call | solution.py:158
  84.2 1.2 %slice.3 = f32[1,1]{1,0:T(1,128)} slice(f32[8,128]{1,0:T(8,128)} %get-tuple-element.5), slice={[0:1], [0:1]} | slice | bytes 8 | tf_op jit(solution)/shard_map/slice | solution.py:178
  85.4 9.4 %convert_bitcast_fusion = (bf16[1,1,3584,256]{3,2,1,0:T(8,128)(2,1)}, f32[3584,256]{1,0:T(8,128)}, f32[1,3584,256]{2,1,0:T(8,128)}) fusion(f32[1,3584,256]{2,1,0:T(8,128)} %param.5, f32[3584,256]{1,0:T(8,128)} %get-tuple-element.6, f32[]{:T(128)} %bitcast.2, f32[1,3584,256]{2,1,0:T(8,128)} %param.3), kind=kLoop, calls=%fused_computation.3 | loop fusion | flops 7340032 | bytes 20185092 | tf_op jit(solution)/shard_map/reshape | solution.py:181

commit v2 on v1

v2 whole, which is shorter than its diff:
```python
import functools
import math

import jax
import jax.numpy as jnp
from jax import lax
from jax.experimental import pallas as pl
from jax.experimental.pallas import tpu as pltpu
from jax.sharding import PartitionSpec as P

MOMENTUM_RATE = 0.9
OUTER_RATE = 0.7
CLIP_LEVEL = 0.2
EPSILON = 1e-06
MESH = pl.DeviceIdType.MESH
SUBS = 4
VMEM_LIMIT = 24 * 1024 * 1024


def device_at(place, n):
    half = n // 2
    up = 2 * place
    down = 2 * (n - 1 - place) + 1
    return jnp.where(place < half, up, down)


def kernel(n, m, subs, max_norm, slow_hbm, fast_hbm, moment_hbm,
           slow_out, moment_out, fast_out,
           ring, slow_ref, fast_ref, moment_ref, pseudo_ref, parts, norms, moment_sem, load_sem, send_sem, recv_sem,
           part_send, part_recv, norm_send, norm_recv):
    rows, cols = slow_ref.shape
    chunk = rows // n
    sub = chunk // subs
    half = cols // 2
    me = lax.axis_index("dp")
    mine = lax.axis_index("mp")
    z, y = me // 2, lax.rem(me, 2)
    place = jnp.where(y == 0, z, n - 1 - z)
    right = device_at(lax.rem(place + 1, n), n)
    left = device_at(lax.rem(place + n - 1, n), n)
    goal = (right, left)
    order = (place, lax.rem(n - place, n))

    def load(d, k):
        c = lax.rem(order[d] - k + n, n)
        at = (pl.ds(pl.multiple_of(c * chunk, chunk), chunk), pl.ds(d * half, half))
        return (
            pltpu.make_async_copy(slow_hbm.at[at], slow_ref.at[at], load_sem.at[0, d, k]),
            pltpu.make_async_copy(fast_hbm.at[at], fast_ref.at[at], load_sem.at[1, d, k]),
        )

    for d in range(2):
        for copy in load(d, 0):
            copy.start()
    barrier = pltpu.get_barrier_semaphore()
    for k in range(1, n):
        pl.semaphore_signal(
            barrier, inc=1, device_id={"dp": lax.rem(me + k, n)}, device_id_type=MESH
        )
    for k in range(1, m):
        pl.semaphore_signal(
            barrier, inc=1, device_id={"mp": lax.rem(mine + k, m)}, device_id_type=MESH
        )
    moment_load = pltpu.make_async_copy(moment_hbm, moment_ref, moment_sem)

    def start_row(c, b):
        return pl.multiple_of(c * chunk + b * sub, sub)

    def own(d, b, c):
        at = (pl.ds(start_row(c, b), sub), pl.ds(d * half, half))
        return slow_ref[at] - fast_ref[at].astype(jnp.float32)

    def reduce_copy(d, b, s):
        return pltpu.make_async_remote_copy(
            src_ref=ring.at[d, b, s], dst_ref=ring.at[d, b, s + 1],
            send_sem=send_sem.at[d, b, s], recv_sem=recv_sem.at[d, b, s],
            device_id={"dp": goal[d]}, device_id_type=MESH,
        )

    def gather_copy(d, b, s, c):
        at = (pl.ds(start_row(c, b), sub), pl.ds(d * half, half))
        return pltpu.make_async_remote_copy(
            src_ref=pseudo_ref.at[at], dst_ref=pseudo_ref.at[at],
            send_sem=send_sem.at[d, b, n - 1 + s], recv_sem=recv_sem.at[d, b, n - 1 + s],
            device_id={"dp": goal[d]}, device_id_type=MESH,
        )

    def part_copy(k):
        return pltpu.make_async_remote_copy(
            src_ref=parts.at[me], dst_ref=parts.at[me],
            send_sem=part_send.at[k], recv_sem=part_recv.at[k],
            device_id={"dp": lax.rem(me + k, n)}, device_id_type=MESH,
        )

    def norm_copy(k):
        return pltpu.make_async_remote_copy(
            src_ref=norms.at[mine], dst_ref=norms.at[mine],
            send_sem=norm_send.at[k], recv_sem=norm_recv.at[k],
            device_id={"mp": lax.rem(mine + k, m)}, device_id_type=MESH,
        )

    streams = [(d, b) for b in range(subs) for d in range(2)]
    for d in range(2):
        for copy in load(d, 0):
            copy.wait()
    for d, b in streams:
        ring[d, b, 0] = own(d, b, order[d])
    pl.semaphore_wait(barrier, n - 1 + m - 1)
    for d, b in streams:
        reduce_copy(d, b, 0).start()
    for k in range(1, n):
        for d in range(2):
            for copy in load(d, k):
                copy.start()
    moment_load.start()

    def reduce_step(s, carry):
        for d in range(2):
            for copy in load(d, s + 1):
                copy.wait()
        for d, b in streams:
            c = lax.rem(order[d] - s - 1 + n, n)
            reduce_copy(d, b, s).wait_recv()
            ring[d, b, s + 1] = ring[d, b, s + 1] + own(d, b, c)
            reduce_copy(d, b, s + 1).start()
        return carry

    lax.fori_loop(0, n - 2, reduce_step, 0)
    for d in range(2):
        for copy in load(d, n - 1):
            copy.wait()
    part = jnp.zeros((8, half), jnp.float32)
    for d, b in streams:
        c = lax.rem(order[d] + 1, n)
        reduce_copy(d, b, n - 2).wait_recv()
        value = (ring[d, b, n - 1] + own(d, b, c)) / n
        pseudo_ref[pl.ds(start_row(c, b), sub), pl.ds(d * half, half)] = value
        gather_copy(d, b, 0, c).start()
        part = part + jnp.sum((value * value).reshape(sub // 8, 8, half), axis=0)
    parts[me] = part

    def gather_step(s, carry):
        for d, b in streams:
            c = lax.rem(order[d] - s + n, n)
            gather_copy(d, b, s, c).wait_recv()
            gather_copy(d, b, s + 1, c).start()
        return carry

    second = (n - 2) // 2
    first = second // 2
    for k in range(1, n):
        part_copy(k).start()
    lax.fori_loop(0, first, gather_step, 0)
    for k in range(1, n):
        part_copy(k).wait_recv()
    norm = parts[0]
    for j in range(1, n):
        norm = norm + parts[j]
    norms[mine] = norm
    for k in range(1, m):
        norm_copy(k).start()
    lax.fori_loop(first, second, gather_step, 0)
    for k in range(1, m):
        norm_copy(k).wait_recv()
    total = norms[0]
    for j in range(1, m):
        total = total + norms[j]
    total = jnp.sum(jnp.sum(total, axis=1, keepdims=True), axis=0, keepdims=True)
    factor = jnp.minimum(1.0, max_norm / (jnp.sqrt(total) + EPSILON))
    moment_load.wait()

    def update(d, c):
        at = (pl.ds(pl.multiple_of(c * chunk, chunk), chunk), pl.ds(d * half, half))
        gradient = factor * pseudo_ref[at]
        moment = MOMENTUM_RATE * moment_ref[at] + gradient
        slow = slow_ref[at] - OUTER_RATE * (gradient + MOMENTUM_RATE * moment)
        moment_out[at] = moment
        slow_out[at] = slow
        fast_out[at] = slow.astype(fast_out.dtype)

    def update_step(s, carry):
        gather_step(s, carry)
        for d in range(2):
            update(d, lax.rem(order[d] - s + n, n))
            update(d, lax.rem(order[d] - (s - second) + n, n))
        return carry

    lax.fori_loop(second, n - 2, update_step, 0)
    for d in range(2):
        update(d, lax.rem(order[d] + 1, n))
    for k in range(1, n):
        part_copy(k).wait_send()
    for k in range(1, m):
        norm_copy(k).wait_send()

    def drain(s, carry):
        for d, b in streams:
            reduce_copy(d, b, s).wait_send()
            gather_copy(d, b, s, 0).wait_send()
        return carry

    lax.fori_loop(0, n - 2, drain, 0)
    for d, b in streams:
        c = lax.rem(order[d] + 2, n)
        reduce_copy(d, b, n - 2).wait_send()
        gather_copy(d, b, n - 2, c).wait()
    for d in range(2):
        update(d, lax.rem(order[d] + 2, n))


def emit_kernel(pieces, *refs):
    count = len(refs) // 2
    sources, targets, sem = refs[:count], refs[count:-1], refs[-1]
    size = sources[0].shape[0] // pieces
    copies = [
        pltpu.make_async_copy(
            sources[i].at[pl.ds(k * size, size)], targets[i].at[pl.ds(k * size, size)], sem.at[i, k]
        )
        for k in range(pieces) for i in range(count)
    ]
    for copy in copies:
        copy.start()
    for copy in copies:
        copy.wait()


def emit(arrays, pieces):
    return pl.pallas_call(
        functools.partial(emit_kernel, pieces),
        out_shape=tuple(jax.ShapeDtypeStruct(x.shape, x.dtype) for x in arrays),
        in_specs=[pl.BlockSpec(memory_space=pltpu.VMEM)] * len(arrays),
        out_specs=tuple(pl.BlockSpec(memory_space=pltpu.HBM) for _ in arrays),
        scratch_shapes=[pltpu.SemaphoreType.DMA((len(arrays), pieces))],
        compiler_params=pltpu.CompilerParams(vmem_limit_bytes=VMEM_LIMIT),
        name="emit",
    )(*arrays)


def body(slow_weights, fast_weights, momentum):
    n, m = lax.axis_size("dp"), lax.axis_size("mp")
    layers, depth, cols = slow_weights.shape
    rows = layers * depth
    max_norm = CLIP_LEVEL * math.sqrt(rows * cols * m)
    subs = SUBS
    while rows % (n * subs * 16):
        subs -= 1
    sub = rows // (n * subs)
    slow = slow_weights.reshape(rows, cols)
    hbm = pl.BlockSpec(memory_space=pltpu.HBM)
    vmem = pl.BlockSpec(memory_space=pltpu.VMEM)
    flat = (slow_weights, fast_weights, momentum)
    flat = [
        pltpu.with_memory_space_constraint(x.reshape(rows, cols), pltpu.HBM) for x in flat
    ]
    results = pl.pallas_call(
        functools.partial(kernel, n, m, subs, max_norm),
        out_shape=(
            jax.ShapeDtypeStruct((rows, cols), jnp.float32),
            jax.ShapeDtypeStruct((rows, cols), jnp.float32),
            jax.ShapeDtypeStruct((rows, cols), jnp.bfloat16),
        ),
        in_specs=[hbm, hbm, hbm],
        out_specs=(vmem, vmem, vmem),
        scratch_shapes=[
            pltpu.VMEM((2, subs, n, sub, cols // 2), jnp.float32),
            pltpu.VMEM((rows, cols), jnp.float32),
            pltpu.VMEM((rows, cols), jnp.bfloat16),
            pltpu.VMEM((rows, cols), jnp.float32),
            pltpu.VMEM((rows, cols), jnp.float32),
            pltpu.VMEM((n, 8, cols // 2), jnp.float32),
            pltpu.VMEM((m, 8, cols // 2), jnp.float32),
            pltpu.SemaphoreType.DMA,
            pltpu.SemaphoreType.DMA((2, 2, n)),
            pltpu.SemaphoreType.DMA((2, subs, 2 * n - 2)),
            pltpu.SemaphoreType.DMA((2, subs, 2 * n - 2)),
            pltpu.SemaphoreType.DMA((n,)),
            pltpu.SemaphoreType.DMA((n,)),
            pltpu.SemaphoreType.DMA((m,)),
            pltpu.SemaphoreType.DMA((m,)),
        ],
        compiler_params=pltpu.CompilerParams(
            collective_id=0, has_side_effects=True, vmem_limit_bytes=VMEM_LIMIT
        ),
        name="ring",
    )(*flat)
    slow_next, momentum_next, fast_next = emit(results, 4)
    return (
        slow_next.reshape(slow_weights.shape),
        momentum_next.reshape(slow_weights.shape),
        fast_next.reshape(fast_weights.shape),
    )


def solution(mesh):
    in_specs = (P(None, None, "mp"), P("dp", None, None, "mp"), P(None, None, "mp"))
    out_specs = (P(None, None, "mp"), P(None, None, "mp"), P("dp", None, None, "mp"))
    return jax.shard_map(body, mesh=mesh, in_specs=in_specs, out_specs=out_specs, check_vma=False)
```

time: 95.1 us -> 83.5 us (0.88)
  other arithmetic: 9.43 us -> 0 us
  local copies, waits for them, and re-layouts: 1.2 us -> 0 us
    reshape x1 -> x0, other arithmetic: 9.43 us -> none  [body(): fast_next = slow_next.astype(jnp.bfloat16).reshape(fast_weights.shape)]
    pallas_call x1, Pallas kernels: 83.6 us -> 79.1 us  [body(): pl.pallas_call(functools.partial(kernel, n, m, subs, max_norm), out_shape...]
    pallas_call x0 -> x1, Pallas kernels: none -> 3.63 us  [emit(): pl.pallas_call(functools.partial(emit_kernel, pieces), out_shape=tuple((j...]
    slice x1 -> x0, local copies, waits for them, and re-layouts: 1.2 us -> none  [body(): gradient = factor[0, 0] * pseudo]
where the time goes in v2:
time: 83.5 us; the launch traced here: 83.4 us
  Pallas kernels  82.7 us (99%)
    pallas_call x1, Pallas kernels, body(): pl.pallas_call(functools.partial(kernel, n, m, subs, max_norm), out_shape...  79.1 us
    pallas_call x1, Pallas kernels, emit(): pl.pallas_call(functools.partial(emit_kernel, pieces), out_shape=tuple((j...  3.63 us

profile of v2, /device:TPU:0, one launch (start us, length us, event | category | flops | bytes accessed | tf_op | source)
XLA Modules:
  0.0 83.4 jit_solution(15759491123640517672)
XLA Ops:
  0.6 79.1 %ring.1 = (f32[3584,256]{1,0:T(8,128)S(1)}, f32[3584,256]{1,0:T(8,128)S(1)}, bf16[3584,256]{1,0:T(8,128)(2,1)S(1)}) custom-call(f32[3584,256]{1,0:T(8,128)} %bitcast.6, bf16[3584,256]{1,0:T(8,128)(2,1)} %bitcast.8, f32[3584,256]{1,0:T(8,128)} %bitcast.7), custom_call_target="tpu_custom_call" | custom-call | tf_op jit(solution)/shard_map/ring/pallas_call | solution.py:255
  79.7 3.6 %emit.1 = (f32[3584,256]{1,0:T(8,128)}, f32[3584,256]{1,0:T(8,128)}, bf16[3584,256]{1,0:T(8,128)(2,1)}) custom-call(f32[3584,256]{1,0:T(8,128)S(1)} %get-tuple-element.9.refs_0_, f32[3584,256]{1,0:T(8,128)S(1)} %get-tuple-element.10.refs_1_, bf16[3584,256]{1,0:T(8,128)(2,1)S(1)} %get-tuple-element.11.refs_2_), custom_call_target="tpu_custom_call" | custom-call | tf_op jit(solution)/shard_map/emit/pallas_call | solution.py:228

commit v3 on v2

--- a/solution.py
+++ b/solution.py
@@ -53,10 +53,8 @@
         for copy in load(d, 0):
             copy.start()
     barrier = pltpu.get_barrier_semaphore()
-    for k in range(1, n):
-        pl.semaphore_signal(
-            barrier, inc=1, device_id={"dp": lax.rem(me + k, n)}, device_id_type=MESH
-        )
+    for other in (left, right):
+        pl.semaphore_signal(barrier, inc=1, device_id={"dp": other}, device_id_type=MESH)
     for k in range(1, m):
         pl.semaphore_signal(
             barrier, inc=1, device_id={"mp": lax.rem(mine + k, m)}, device_id_type=MESH
@@ -105,7 +103,7 @@
             copy.wait()
     for d, b in streams:
         ring[d, b, 0] = own(d, b, order[d])
-    pl.semaphore_wait(barrier, n - 1 + m - 1)
+    pl.semaphore_wait(barrier, 2 + m - 1)
     for d, b in streams:
         reduce_copy(d, b, 0).start()
     for k in range(1, n):

time: 83.5 us -> 82 us (0.982)
  Pallas kernels: 82.7 us -> 81.2 us
    pallas_call x1, Pallas kernels: 79.1 us -> 77.6 us  [body(): pl.pallas_call(functools.partial(kernel, n, m, subs, max_norm), out_shape...]
where the time goes in v3:
time: 82 us; the launch traced here: 81.9 us
  Pallas kernels  81.2 us (99%)
    pallas_call x1, Pallas kernels, body(): pl.pallas_call(functools.partial(kernel, n, m, subs, max_norm), out_shape...  77.6 us
    pallas_call x1, Pallas kernels, emit(): pl.pallas_call(functools.partial(emit_kernel, pieces), out_shape=tuple((j...  3.63 us

profile of v3, /device:TPU:0, one launch (start us, length us, event | category | flops | bytes accessed | tf_op | source)
XLA Modules:
  0.0 81.9 jit_solution(11387892964132624767)
XLA Ops:
  0.6 77.6 %ring.1 = (f32[3584,256]{1,0:T(8,128)S(1)}, f32[3584,256]{1,0:T(8,128)S(1)}, bf16[3584,256]{1,0:T(8,128)(2,1)S(1)}) custom-call(f32[3584,256]{1,0:T(8,128)} %bitcast.6, bf16[3584,256]{1,0:T(8,128)(2,1)} %bitcast.8, f32[3584,256]{1,0:T(8,128)} %bitcast.7), custom_call_target="tpu_custom_call" | custom-call | tf_op jit(solution)/shard_map/ring/pallas_call | solution.py:253
  78.3 3.6 %emit.1 = (f32[3584,256]{1,0:T(8,128)}, f32[3584,256]{1,0:T(8,128)}, bf16[3584,256]{1,0:T(8,128)(2,1)}) custom-call(f32[3584,256]{1,0:T(8,128)S(1)} %get-tuple-element.9.refs_0_, f32[3584,256]{1,0:T(8,128)S(1)} %get-tuple-element.10.refs_1_, bf16[3584,256]{1,0:T(8,128)(2,1)S(1)} %get-tuple-element.11.refs_2_), custom_call_target="tpu_custom_call" | custom-call | tf_op jit(solution)/shard_map/emit/pallas_call | solution.py:226

commit v4 on v3

--- a/solution.py
+++ b/solution.py
@@ -98,18 +98,17 @@
         )
 
     streams = [(d, b) for b in range(subs) for d in range(2)]
-    for d in range(2):
-        for copy in load(d, 0):
-            copy.wait()
-    for d, b in streams:
-        ring[d, b, 0] = own(d, b, order[d])
-    pl.semaphore_wait(barrier, 2 + m - 1)
-    for d, b in streams:
-        reduce_copy(d, b, 0).start()
     for k in range(1, n):
         for d in range(2):
             for copy in load(d, k):
                 copy.start()
+    for d in range(2):
+        for copy in load(d, 0):
+            copy.wait()
+    pl.semaphore_wait(barrier, 2 + m - 1)
+    for d, b in streams:
+        ring[d, b, 0] = own(d, b, order[d])
+        reduce_copy(d, b, 0).start()
     moment_load.start()
 
     def reduce_step(s, carry):
@@ -167,8 +166,8 @@
     factor = jnp.minimum(1.0, max_norm / (jnp.sqrt(total) + EPSILON))
     moment_load.wait()
 
-    def update(d, c):
-        at = (pl.ds(pl.multiple_of(c * chunk, chunk), chunk), pl.ds(d * half, half))
+    def update(d, c, start=0, size=chunk):
+        at = (pl.ds(pl.multiple_of(c * chunk + start, 16), size), pl.ds(d * half, half))
         gradient = factor * pseudo_ref[at]
         moment = MOMENTUM_RATE * moment_ref[at] + gradient
         slow = slow_ref[at] - OUTER_RATE * (gradient + MOMENTUM_RATE * moment)
@@ -202,8 +201,7 @@
         c = lax.rem(order[d] + 2, n)
         reduce_copy(d, b, n - 2).wait_send()
         gather_copy(d, b, n - 2, c).wait()
-    for d in range(2):
-        update(d, lax.rem(order[d] + 2, n))
+        update(d, c, b * sub, sub)
 
 
 def emit_kernel(pieces, *refs):

time: 82 us -> 81.9 us (level)
  no operation moved by 1% of the time
where the time goes in v4:
time: 81.9 us; the launch traced here: 81.7 us
  Pallas kernels  81.1 us (99%)
    pallas_call x1, Pallas kernels, body(): pl.pallas_call(functools.partial(kernel, n, m, subs, max_norm), out_shape...  77.5 us
    pallas_call x1, Pallas kernels, emit(): pl.pallas_call(functools.partial(emit_kernel, pieces), out_shape=tuple((j...  3.63 us

profile of v4, /device:TPU:0, one launch (start us, length us, event | category | flops | bytes accessed | tf_op | source)
XLA Modules:
  0.0 81.7 jit_solution(1748748784282840822)
XLA Ops:
  0.6 77.5 %ring.1 = (f32[3584,256]{1,0:T(8,128)S(1)}, f32[3584,256]{1,0:T(8,128)S(1)}, bf16[3584,256]{1,0:T(8,128)(2,1)S(1)}) custom-call(f32[3584,256]{1,0:T(8,128)} %bitcast.6, bf16[3584,256]{1,0:T(8,128)(2,1)} %bitcast.8, f32[3584,256]{1,0:T(8,128)} %bitcast.7), custom_call_target="tpu_custom_call" | custom-call | tf_op jit(solution)/shard_map/ring/pallas_call | solution.py:251
  78.1 3.6 %emit.1 = (f32[3584,256]{1,0:T(8,128)}, f32[3584,256]{1,0:T(8,128)}, bf16[3584,256]{1,0:T(8,128)(2,1)}) custom-call(f32[3584,256]{1,0:T(8,128)S(1)} %get-tuple-element.9.refs_0_, f32[3584,256]{1,0:T(8,128)S(1)} %get-tuple-element.10.refs_1_, bf16[3584,256]{1,0:T(8,128)(2,1)S(1)} %get-tuple-element.11.refs_2_), custom_call_target="tpu_custom_call" | custom-call | tf_op jit(solution)/shard_map/emit/pallas_call | solution.py:224
